TPU v7x, 16 devices: a whole 2x2x2 slice. The times are simulated.
16 devices in a mesh: rep: 1, r: 2 (over z), s: 8 (over x, y, core).
Axes of the slice: x: 2, y: 2, z: 2, core: 2. Of those that a mesh axis runs over, the one named last changes fastest.
Arguments:
- x: bfloat16 [16, 2048, 1024], P(('rep', 'r', 's'))
- dy: bfloat16 [16, 2048, 1024], P(('rep', 'r', 's'))
- w_gate: bfloat16 [2, 1024, 3200], P(None, 's')
- w_up: bfloat16 [2, 1024, 3200], P(None, 's')
- w_down: bfloat16 [2, 3200, 1024], P(None, 's')
Outputs:
- output 1: bfloat16 [16, 2048, 1024], P(('rep', 'r', 's'))
- output 2: bfloat16 [2, 1024, 3200], P('rep', 's')
- output 3: bfloat16 [2, 1024, 3200], P('rep', 's')
- output 4: bfloat16 [2, 3200, 1024], P('rep', 's')
All inputs are finite; a program needn't handle non-finite values.
Results may differ from a plain program's by a relative error of at most 0.018.
Values are sent between devices in bfloat16 or wider.
A program may use at most 2 GiB of HBM per device.

v0:
```python
import jax
import jax.numpy as jnp
from jax import lax
from jax.sharding import PartitionSpec as P

NAMES = ("w_gate", "w_up", "w_down")


def matmul(a, w):
    return jnp.dot(a, w, preferred_element_type=jnp.float32).astype(jnp.bfloat16)


def normed(h):
    wide = h.astype(jnp.float32)
    scale = lax.rsqrt(jnp.mean(wide**2, -1, keepdims=True) + 1e-6)
    return (wide * scale).astype(jnp.bfloat16)


def layer(h, w):
    a = normed(h)
    gate = jnp.dot(a, w["w_gate"], preferred_element_type=jnp.float32)
    up = jnp.dot(a, w["w_up"], preferred_element_type=jnp.float32)
    return h + matmul((jax.nn.silu(gate) * up).astype(jnp.bfloat16), w["w_down"])


def solution(mesh):
    def fetched(weights, number):
        return {name: lax.all_gather(w[number], "s", axis=0, tiled=True) for name, w in zip(NAMES, weights, strict=True)}

    def summed(term):
        return lax.psum(lax.psum_scatter(term, "s", scatter_dimension=0, tiled=True), "r")

    def step(x, dy, *weights):
        layers = weights[0].shape[0]
        h, inputs = x[0], []
        for number in range(layers):
            inputs.append(h)
            h = layer(h, fetched(weights, number))
        by_h, mine = dy[0], [None] * layers
        for number in reversed(range(layers)):
            _, back = jax.vjp(lambda w, h: layer(h, w), fetched(weights, number), inputs[number])
            by_w, by_h = back(by_h)
            mine[number] = [summed(by_w[name]) for name in NAMES]
        return (by_h[None], *(jnp.stack([mine[number][i] for number in range(layers)]) for i in range(3)))

    states, cut = P(("rep", "r", "s"), None, None), P(None, "s", None)
    return jax.shard_map(
        step,
        mesh=mesh,
        in_specs=(states, states) + (cut,) * 3,
        out_specs=(states,) + (P("rep", "s", None),) * 3,
        check_vma=False,
    )
```

profile of v0, /device:TPU:0, one launch (start us, length us, event | category | flops | bytes accessed | tf_op | source)
XLA Modules:
  0.0 881.1 jit_solution(1703158247103631940)
XLA Ops:
  7.2 2.8 fusion.68
  10.1 2.7 fusion.69
  12.8 1.3 fusion.70
  14.2 0.5 all-gather.21.cloned.1.call-update
  14.8 0.5 all-gather.23.cloned.1.call-update
  15.4 0.5 all-gather.19.cloned.1.call-update
  16.0 6.4 copy.10
  22.4 3.1 fusion.15
  25.5 0.6 copy-done.7
  26.1 6.5 copy.9
  32.6 23.1 %all-gather.13.cloned.1.call-done = bf16[1,1024,3200]{2,1,0:T(8,128)(2,1)} async-done(((bf16[1,128,3200]{2,1,0:T(8,128)(2,1)}), bf16[1,1024,3200]{2,1,0:T(8,128)(2,1)}) %all-gather.13.cloned.1.call-update) | async-done | bytes 6553616 | tf_op jit(solution)/shard_map/all_gather | solution.py:28
  55.7 22.9 %fusion.40 = f32[2048,3200]{1,0:T(8,128)} fusion(bf16[1,1024,3200]{2,1,0:T(8,128)(2,1)} %all-gather.13.cloned.1.call-done, bf16[1,2048,1024]{1,2,0:T(8,128)(2,1)} %copy.10, f32[2048]{0:T(1024)S(1)} %fusion.61), kind=kOutput, calls=%fused_computation.65 | convolution fusion | flops 13428064256 | bytes 36970496 | tf_op jit(solution)/shard_map/dot_general | solution.py:21
  78.6 21.4 %all-gather.15.cloned.1.call-done = bf16[1,1024,3200]{2,1,0:T(8,128)(2,1)} async-done(((bf16[1,128,3200]{2,1,0:T(8,128)(2,1)}), bf16[1,1024,3200]{2,1,0:T(8,128)(2,1)}) %all-gather.15.cloned.1.call-update) | async-done | bytes 6553616 | tf_op jit(solution)/shard_map/all_gather | solution.py:28
  100.0 31.4 %multiply_convert_fusion.1 = (bf16[2048,3200]{1,0:T(8,128)(2,1)}, f32[2048,3200]{1,0:T(8,128)}) fusion(f32[2048,3200]{1,0:T(8,128)} %fusion.40, bf16[1,1024,3200]{2,1,0:T(8,128)(2,1)} %all-gather.15.cloned.1.call-done, bf16[1,2048,1024]{1,2,0:T(8,128)(2,1)} %copy.10, f32[2048]{0:T(1024)S(1)} %fusion.61), kind=kOutput, calls=%fused_computation.13 | convolution fusion | flops 13467385856 | bytes 76292096 | tf_op jit(solution)/shard_map/dot_general | solution.py:22
  131.4 12.9 %all-gather.17.cloned.1.call-done = bf16[1,3200,1024]{2,1,0:T(8,128)(2,1)} async-done(((bf16[1,400,1024]{2,1,0:T(8,128)(2,1)}), bf16[1,3200,1024]{2,1,0:T(8,128)(2,1)}) %all-gather.17.cloned.1.call-update) | async-done | bytes 6553616 | tf_op jit(solution)/shard_map/all_gather | solution.py:28
  144.4 21.9 %fusion.18 = (f32[2048]{0:T(1024)S(1)}, bf16[2048,1024]{0,1:T(8,128)(2,1)}) fusion(bf16[2048,3200]{1,0:T(8,128)(2,1)} %get-tuple-element.20, bf16[1,3200,1024]{2,1,0:T(8,128)(2,1)} %all-gather.17.cloned.1.call-done, bf16[1,2048,1024]{1,2,0:T(8,128)(2,1)} %copy.10), kind=kOutput, calls=%fused_computation.40 | convolution fusion | flops 13432256512 | bytes 28057600 | tf_op jit(solution)/shard_map/dot_general | solution.py:10
  166.3 22.3 %all-gather.21.cloned.1.call-done = bf16[1,3200,1024]{2,1,0:T(8,128)(2,1)} async-done(((bf16[1,400,1024]{2,1,0:T(8,128)(2,1)}), bf16[1,3200,1024]{2,1,0:T(8,128)(2,1)}) %all-gather.21.cloned.1.call-update) | async-done | bytes 6553616 | tf_op jit(solution)/shard_map/all_gather | solution.py:28
  188.6 21.1 %convolution_convert_fusion.1 = bf16[2048,3200]{1,0:T(8,128)(2,1)} fusion(bf16[1,3200,1024]{2,1,0:T(8,128)(2,1)} %all-gather.21.cloned.1.call-done, bf16[1,2048,1024]{2,1,0:T(8,128)(2,1)} %param.6), kind=kOutput, calls=%fused_computation.21 | convolution fusion | flops 13428326400 | bytes 23855104 | tf_op jit(solution)/shard_map/transpose(jvp())/dot_general | solution.py:10
  209.7 23.6 %all-gather.23.cloned.1.call-done = bf16[1,1024,3200]{2,1,0:T(8,128)(2,1)} async-done(((bf16[1,128,3200]{2,1,0:T(8,128)(2,1)}), bf16[1,1024,3200]{2,1,0:T(8,128)(2,1)}) %all-gather.23.cloned.1.call-update) | async-done | bytes 6553616 | tf_op jit(solution)/shard_map/all_gather | solution.py:28
  233.3 22.8 %fusion.24 = f32[2048,3200]{1,0:T(8,128)} fusion(bf16[1,1024,3200]{2,1,0:T(8,128)(2,1)} %all-gather.23.cloned.1.call-done, bf16[2048,1024]{0,1:T(8,128)(2,1)} %get-tuple-element.23, f32[2048]{0:T(1024)S(1)} %fusion.62), kind=kOutput, calls=%fused_computation.49 | convolution fusion | flops 13428064256 | bytes 36970496 | tf_op jit(solution)/shard_map/jvp()/dot_general | solution.py:22
  256.1 22.0 %all-gather.19.cloned.1.call-done = bf16[1,1024,3200]{2,1,0:T(8,128)(2,1)} async-done(((bf16[1,128,3200]{2,1,0:T(8,128)(2,1)}), bf16[1,1024,3200]{2,1,0:T(8,128)(2,1)}) %all-gather.19.cloned.1.call-update) | async-done | bytes 6553616 | tf_op jit(solution)/shard_map/all_gather | solution.py:28
  278.1 38.5 %fusion.1 = (bf16[2048,3200]{1,0:T(8,128)(2,1)}, f32[2048,3200]{1,0:T(8,128)}) fusion(f32[2048,3200]{1,0:T(8,128)} %fusion.24, bf16[2048,3200]{1,0:T(8,128)(2,1)} %convolution_convert_fusion.1, bf16[1,1024,3200]{2,1,0:T(8,128)(2,1)} %all-gather.19.cloned.1.call-done, bf16[2048,1024]{0,1:T(8,128)(2,1)} %get-tuple-element.23, f32[2048]{0:T(1024)S(1)} %fusion.62), kind=kOutput, calls=%fused_computation.7 | convolution fusion | flops 13506707456 | bytes 89399296 | tf_op jit(solution)/shard_map/jvp()/dot_general | solution.py:21
  316.6 22.6 %fusion.7 = bf16[2048,1024]{0,1:T(8,128)(2,1)} fusion(bf16[2048,3200]{1,0:T(8,128)(2,1)} %convolution_convert_fusion.1, bf16[1,1024,3200]{2,1,0:T(8,128)(2,1)} %all-gather.23.cloned.1.call-done, f32[2048,3200]{1,0:T(8,128)} %get-tuple-element.25), kind=kOutput, calls=%fused_computation.17 | convolution fusion | flops 13461094400 | bytes 50069504 | tf_op jit(solution)/shard_map/transpose(jvp())/dot_general | solution.py:22
  339.2 21.9 %fusion.20 = (f32[2048]{0:T(1024)S(1)}, bf16[2048,1024]{0,1:T(8,128)(2,1)}) fusion(bf16[2048,1024]{0,1:T(8,128)(2,1)S(1)} %copy-done.5, bf16[2048,1024]{0,1:T(8,128)(2,1)} %fusion.7, bf16[2048,3200]{1,0:T(8,128)(2,1)} %get-tuple-element.24, bf16[1,1024,3200]{2,1,0:T(8,128)(2,1)} %all-gather.19.cloned.1.call-done), kind=kOutput, calls=%fused_computation.42 | convolution fusion | flops 13432256512 | bytes 32251904 | tf_op jit(solution)/shard_map/transpose(jvp())/dot_general | solution.py:21
  361.1 4.9 fusion.44
  366.0 2.0 copy-done.2
  367.9 19.5 %convolution_convert_fusion.2 = bf16[3200,1024]{1,0:T(8,128)(2,1)} fusion(bf16[2048,3200]{1,0:T(8,128)(2,1)} %get-tuple-element.20, bf16[2048,1024]{0,1:T(8,128)(2,1)S(1)} %fusion.44), kind=kOutput, calls=%fused_computation.46 | convolution fusion | flops 13425049600 | bytes 23855104 | tf_op jit(solution)/shard_map/transpose(jvp())/dot_general | solution.py:10
  387.4 0.0 reduce-scatter.17.cloned.1.call-start
  387.5 26.2 %fusion.21 = bf16[3200,1024]{1,0:T(8,128)(2,1)} fusion(f32[2048,3200]{1,0:T(8,128)} %fusion.24, bf16[1,2048,1024]{2,1,0:T(8,128)(2,1)} %param.6, f32[2048,3200]{1,0:T(8,128)} %get-tuple-element.25), kind=kOutput, calls=%fused_computation.43 | convolution fusion | flops 13464371200 | bytes 63176704 | tf_op jit(solution)/shard_map/transpose(jvp())/dot_general | solution.py:10
  413.7 0.0 reduce-scatter.11.cloned.1.call-start
  413.8 39.3 %fusion.3 = (bf16[2048,3200]{1,0:T(8,128)(2,1)}, bf16[2048,3200]{1,0:T(8,128)(2,1)}) fusion(f32[2048,3200]{1,0:T(8,128)} %fusion.40, f32[2048,3200]{1,0:T(8,128)} %get-tuple-element.21, bf16[2048,1024]{0,1:T(8,128)(2,1)} %copy-done.2, bf16[1,3200,1024]{2,1,0:T(8,128)(2,1)} %all-gather.17.cloned.1.call-done), kind=kOutput, calls=%fused_computation.9 | convolution fusion | flops 13506969600 | bytes 89391104 | tf_op jit(solution)/shard_map/transpose(jvp())/dot_general | solution.py:10
  453.1 24.1 %fusion.22 = bf16[1024,3200]{1,0:T(8,128)(2,1)} fusion(bf16[2048,3200]{1,0:T(8,128)(2,1)} %get-tuple-element.29, bf16[1,2048,1024]{1,2,0:T(8,128)(2,1)S(1)} %copy-done, f32[2048]{0:T(1024)S(1)} %copy-done.10, f32[2048,3200]{1,0:T(8,128)} %fusion.40), kind=kOutput, calls=%fused_computation.44 | convolution fusion | flops 13470662656 | bytes 50077696 | tf_op jit(solution)/shard_map/transpose(jvp())/dot_general | solution.py:22
  477.2 0.0 reduce-scatter.13.cloned.1.call-start
  477.3 25.4 %fusion.23 = bf16[1024,3200]{1,0:T(8,128)(2,1)} fusion(bf16[2048,3200]{1,0:T(8,128)(2,1)} %convolution_convert_fusion.1, bf16[2048,1024]{0,1:T(8,128)(2,1)} %get-tuple-element.23, f32[2048]{0:T(1024)S(1)} %copy-done.12, f32[2048,3200]{1,0:T(8,128)} %get-tuple-element.25), kind=kOutput, calls=%fused_computation.45 | convolution fusion | flops 13470662656 | bytes 50077696 | tf_op jit(solution)/shard_map/transpose(jvp())/dot_general | solution.py:22
  502.8 21.0 %convolution_convert_fusion.3 = bf16[1024,3200]{1,0:T(8,128)(2,1)} fusion(bf16[2048,3200]{1,0:T(8,128)(2,1)} %get-tuple-element.24, bf16[2048,1024]{0,1:T(8,128)(2,1)} %get-tuple-element.23, f32[2048]{0:T(1024)S(1)} %copy-done.12), kind=kOutput, calls=%fused_computation.47 | convolution fusion | flops 13428064256 | bytes 23863296 | tf_op jit(solution)/shard_map/transpose(jvp())/dot_general | solution.py:21
  523.9 0.0 reduce-scatter.7.cloned.1.call-start
  523.9 21.1 %convolution_convert_fusion.4 = bf16[1024,3200]{1,0:T(8,128)(2,1)} fusion(bf16[2048,3200]{1,0:T(8,128)(2,1)} %get-tuple-element.28, bf16[1,2048,1024]{1,2,0:T(8,128)(2,1)} %copy.10, f32[2048]{0:T(1024)S(1)} %copy-done.10), kind=kOutput, calls=%fused_computation.48 | convolution fusion | flops 13428064256 | bytes 23863296 | tf_op jit(solution)/shard_map/transpose(jvp())/dot_general | solution.py:21
  545.1 19.5 %reduce-scatter.11.cloned.1.call-done = bf16[128,3200]{1,0:T(8,128)(2,1)} async-done(((bf16[1024,3200]{1,0:T(8,128)(2,1)}), bf16[128,3200]{1,0:T(8,128)(2,1)}) %reduce-scatter.11.cloned.1.call-update) | async-done | bytes 819216 | tf_op jit(solution)/shard_map/reduce_scatter | solution.py:31
  564.6 60.0 %reduce-scatter.13.cloned.1.call-done = bf16[128,3200]{1,0:T(8,128)(2,1)} async-done(((bf16[1024,3200]{1,0:T(8,128)(2,1)}), bf16[128,3200]{1,0:T(8,128)(2,1)}) %reduce-scatter.13.cloned.1.call-update) | async-done | bytes 819216 | tf_op jit(solution)/shard_map/reduce_scatter | solution.py:31
  624.6 60.1 %reduce-scatter.9.cloned.1.call-done = bf16[128,3200]{1,0:T(8,128)(2,1)} async-done(((bf16[1024,3200]{1,0:T(8,128)(2,1)}), bf16[128,3200]{1,0:T(8,128)(2,1)}) %reduce-scatter.9.cloned.1.call-update) | async-done | bytes 819216 | tf_op jit(solution)/shard_map/reduce_scatter | solution.py:31
  684.7 60.0 %reduce-scatter.7.cloned.1.call-done = bf16[128,3200]{1,0:T(8,128)(2,1)} async-done(((bf16[1024,3200]{1,0:T(8,128)(2,1)}), bf16[128,3200]{1,0:T(8,128)(2,1)}) %reduce-scatter.7.cloned.1.call-update) | async-done | bytes 819216 | tf_op jit(solution)/shard_map/reduce_scatter | solution.py:31
  744.8 22.9 %fusion.9 = bf16[2048,1024]{0,1:T(8,128)(2,1)} fusion(bf16[2048,3200]{1,0:T(8,128)(2,1)} %get-tuple-element.29, bf16[1,1024,3200]{2,1,0:T(8,128)(2,1)} %all-gather.15.cloned.1.call-done, f32[2048,3200]{1,0:T(8,128)} %fusion.40), kind=kOutput, calls=%fused_computation.19 | convolution fusion | flops 13461094400 | bytes 50069504 | tf_op jit(solution)/shard_map/transpose(jvp())/dot_general | solution.py:22
  767.7 19.7 %fusion.17 = (f32[2048]{0:T(1024)S(1)}, bf16[2048,1024]{0,1:T(8,128)(2,1)S(1)}) fusion(bf16[1,2048,1024]{1,2,0:T(8,128)(2,1)S(1)} %copy-done.1, bf16[2048,1024]{0,1:T(8,128)(2,1)} %fusion.9, bf16[2048,3200]{1,0:T(8,128)(2,1)} %get-tuple-element.28, bf16[1,1024,3200]{2,1,0:T(8,128)(2,1)} %all-gather.13.cloned.1.call-done), kind=kOutput, calls=%fused_computation.39 | convolution fusion | flops 13432256512 | bytes 32251904 | tf_op jit(solution)/shard_map/transpose(jvp())/dot_general | solution.py:21
  787.4 4.8 fusion.43
  792.2 6.4 copy.11
  798.6 68.9 %all-reduce.3.cloned.1.call-done = (bf16[1,128,3200]{2,1,0:T(8,128)(2,1)}, bf16[1,128,3200]{2,1,0:T(8,128)(2,1)}, bf16[1,128,3200]{2,1,0:T(8,128)(2,1)}, bf16[1,...) async-done(((bf16[1,128,3200]{2,1,0:T(8,128)(2,1)}, bf16[1,128,3200]{2,1,0:T(8,128)(2,1)}, bf16[1,128,3200]{2,1,0:T(8,128)(2,1)}, ...) | async-done | bytes 4915216 | tf_op jit(solution)/shard_map/psum | solution.py:31
  867.5 2.7 pad_maximum_fusion.2
  870.2 3.9 pad_maximum_fusion
  (53 shorter events, 0.7 us)
Async XLA Ops:
  7.2 5.7 copy-start.6
  7.2 48.5 %all-gather.13.cloned.1.call-start = ((), (), s32[]{:S(2)}) async-start(), calls=%async_computation.12 | async-start | bytes 7372800 | tf_op jit(solution)/shard_map/all_gather | solution.py:28
  10.0 90.0 %all-gather.15.cloned.1.call-start = ((), (), s32[]{:S(2)}) async-start(), calls=%async_computation.13 | async-start | bytes 7372800 | tf_op jit(solution)/shard_map/all_gather | solution.py:28
  12.8 131.6 %all-gather.17.cloned.1.call-start = ((), (), s32[]{:S(2)}) async-start(), calls=%async_computation.14 | async-start | bytes 7372800 | tf_op jit(solution)/shard_map/all_gather | solution.py:28
  14.2 174.4 %all-gather.21.cloned.1.call-start = ((), (), s32[]{:S(2)}) async-start(), calls=%async_computation.16 | async-start | bytes 7372800 | tf_op jit(solution)/shard_map/all_gather | solution.py:28
  14.8 218.5 %all-gather.23.cloned.1.call-start = ((), (), s32[]{:S(2)}) async-start(), calls=%async_computation.17 | async-start | bytes 7372800 | tf_op jit(solution)/shard_map/all_gather | solution.py:28
  15.4 262.7 %all-gather.19.cloned.1.call-start = ((), (), s32[]{:S(2)}) async-start(), calls=%async_computation.15 | async-start | bytes 7372800 | tf_op jit(solution)/shard_map/all_gather | solution.py:28
  15.9 529.1 %reduce-scatter.15.cloned.1.call-start = ((), (), s32[]{:S(2)}) async-start(), calls=%async_computation.10 | async-start | bytes 7372800 | tf_op jit(solution)/shard_map/reduce_scatter | solution.py:31
  25.5 0.6 copy-start.7
  26.1 74.0 %copy-start.9 = (f32[2048]{0:T(1024)}, f32[2048]{0:T(1024)S(1)}, u32[]{:S(2)}) copy-start(f32[2048]{0:T(1024)S(1)} %fusion.61) | copy-start | bytes 24580
  166.3 43.4 %copy-start.13 = (f32[2048]{0:T(1024)}, f32[2048]{0:T(1024)S(1)}, u32[]{:S(2)}) copy-start(f32[2048]{0:T(1024)S(1)} %get-tuple-element.22) | copy-start | bytes 24580
  166.3 194.8 %copy-start.11 = (f32[2048]{0:T(1024)}, f32[2048]{0:T(1024)S(1)}, u32[]{:S(2)}) copy-start(f32[2048]{0:T(1024)S(1)} %fusion.62) | copy-start | bytes 24580
  316.6 22.6 %copy-start.5 = (bf16[2048,1024]{0,1:T(8,128)(2,1)S(1)}, bf16[2048,1024]{0,1:T(8,128)(2,1)}, u32[]{:S(2)}) copy-start(bf16[2048,1024]{0,1:T(8,128)(2,1)} %get-tuple-element.23) | copy-start | bytes 12582916
  339.2 21.9 %copy-start.14 = (f32[2048]{0:T(1024)S(1)}, f32[2048]{0:T(1024)}, u32[]{:S(2)}) copy-start(f32[2048]{0:T(1024)} %copy-done.13) | copy-start | bytes 24580
  339.2 21.9 %copy-start.4 = (bf16[1,2048,1024]{1,2,0:T(8,128)(2,1)S(1)}, bf16[1,2048,1024]{1,2,0:T(8,128)(2,1)}, u32[]{:S(2)}) copy-start(bf16[1,2048,1024]{1,2,0:T(8,128)(2,1)} %copy.9) | copy-start | bytes 12582916
  366.0 2.0 copy-start.2
  387.4 157.6 %reduce-scatter.17.cloned.1.call-start = ((), (), s32[]{:S(2)}) async-start(), calls=%async_computation.11 | async-start | bytes 7372800 | tf_op jit(solution)/shard_map/reduce_scatter | solution.py:31
  413.7 150.9 %reduce-scatter.11.cloned.1.call-start = ((), (), s32[]{:S(2)}) async-start(), calls=%async_computation.8 | async-start | bytes 7372800 | tf_op jit(solution)/shard_map/reduce_scatter | solution.py:31
  413.7 39.4 %copy-start = (bf16[1,2048,1024]{1,2,0:T(8,128)(2,1)S(1)}, bf16[1,2048,1024]{1,2,0:T(8,128)(2,1)}, u32[]{:S(2)}) copy-start(bf16[1,2048,1024]{1,2,0:T(8,128)(2,1)} %copy.10) | copy-start | bytes 12582916
  413.8 39.3 %copy-start.10 = (f32[2048]{0:T(1024)S(1)}, f32[2048]{0:T(1024)}, u32[]{:S(2)}) copy-start(f32[2048]{0:T(1024)} %copy-done.9) | copy-start | bytes 24580
  453.1 24.2 %copy-start.12 = (f32[2048]{0:T(1024)S(1)}, f32[2048]{0:T(1024)}, u32[]{:S(2)}) copy-start(f32[2048]{0:T(1024)} %copy-done.11) | copy-start | bytes 24580
  477.2 147.4 %reduce-scatter.13.cloned.1.call-start = ((), (), s32[]{:S(2)}) async-start(), calls=%async_computation.9 | async-start | bytes 7372800 | tf_op jit(solution)/shard_map/reduce_scatter | solution.py:31
  502.8 182.0 %reduce-scatter.9.cloned.1.call-start = ((), (), s32[]{:S(2)}) async-start(), calls=%async_computation.7 | async-start | bytes 7372800 | tf_op jit(solution)/shard_map/reduce_scatter | solution.py:31
  523.9 220.9 %reduce-scatter.7.cloned.1.call-start = ((), (), s32[]{:S(2)}) async-start(), calls=%async_computation.6 | async-start | bytes 7372800 | tf_op jit(solution)/shard_map/reduce_scatter | solution.py:31
  545.0 322.5 %all-reduce.3.cloned.1.call-start = ((), (), s32[]{:S(2)}) async-start(), calls=%async_computation.18 | async-start | bytes 9830400 | tf_op jit(solution)/shard_map/psum | solution.py:31
  744.8 22.9 %copy-start.1 = (bf16[1,2048,1024]{1,2,0:T(8,128)(2,1)S(1)}, bf16[1,2048,1024]{1,2,0:T(8,128)(2,1)}, u32[]{:S(2)}) copy-start(bf16[1,2048,1024]{1,2,0:T(8,128)(2,1)} %copy.10) | copy-start | bytes 12582916
  767.7 19.8 %copy-start.8 = (f32[2048]{0:T(1024)S(1)}, f32[2048]{0:T(1024)}, u32[]{:S(2)}) copy-start(f32[2048]{0:T(1024)} %copy-done.7) | copy-start | bytes 24580
  767.7 19.8 %copy-start.3 = (bf16[2048,1024]{0,1:T(8,128)(2,1)S(1)}, bf16[2048,1024]{0,1:T(8,128)(2,1)}, u32[]{:S(2)}) copy-start(bf16[2048,1024]{0,1:T(8,128)(2,1)} %copy-done.2) | copy-start | bytes 12582916
Sparse Core Ops, SparseCore 0:
  10.4 45.2 all-gather.12
  57.5 42.4 all-gather.14
  101.9 42.4 all-gather.16
  146.1 42.4 all-gather.20
  190.8 42.4 all-gather.22
  235.6 42.4 all-gather.18
  387.6 56.6 reduce-scatter.14
  447.7 56.6 reduce-scatter.16
  507.9 56.6 reduce-scatter.10
  567.9 56.6 reduce-scatter.12
  628.0 56.6 reduce-scatter.8
  688.0 56.6 reduce-scatter.6
  747.9 119.5 all-reduce.2
where the time goes:
time: 889 us; the launch traced here: 881 us
  matrix products  422 us (47%)
  waiting for transfers between devices  396 us (45%)
  local copies, waits for them, and re-layouts  28.7 us (3%)
  other arithmetic  19.4 us (2%)
  between operations  14.5 us (2%)
    reduce_scatter x6, waiting for transfers between devices, summed(): lax.psum_scatter(term, 's', scatter_dimension=0, tiled=True)  200 us
    dot_general x6, matrix products, layer(): up = jnp.dot(a, w['w_up'], preferred_element_type=jnp.float32)  149 us
    dot_general x6, matrix products, layer(): gate = jnp.dot(a, w['w_gate'], preferred_element_type=jnp.float32)  145 us
    dot_general x5, matrix products, matmul(): jnp.dot(a, w, preferred_element_type=jnp.float32).astype(jnp.bfloat16)  128 us
    all_gather x6, waiting for transfers between devices, fetched(): lax.all_gather(w[number], 's', axis=0, tiled=True)  125 us
    psum x1, waiting for transfers between devices, summed(): lax.psum(lax.psum_scatter(term, 's', scatter_dimension=0, tiled=True), 'r')  68.9 us
    unnamed x33, local copies, waits for them, and re-layouts  21.9 us
  transfers between devices with their start and end apart: 13, of which 11 were waited for; matrix products, arithmetic and copies ran while one was open for 40% of the time, Pallas kernels for 0%

commit v1 on v0

v1 whole, which is shorter than its diff:
```python
import jax
import jax.numpy as jnp
from jax import lax
from jax.experimental import pallas as pl
from jax.experimental.pallas import tpu as pltpu
from jax.sharding import PartitionSpec as P

BF, F32 = jnp.bfloat16, jnp.float32
MESH = pl.DeviceIdType.MESH
T, D, F = 2048, 1024, 3200
FT, NF = 640, 5
W2 = 2 * FT
CA, CB = 3 * W2, 2 * W2


def dot(a, b, contract=((1,), (0,))):
    return lax.dot_general(a, b, (contract, ((), ())), preferred_element_type=F32)


def normed(h):
    wide = h.astype(F32)
    return (wide * lax.rsqrt(jnp.mean(wide * wide, -1, keepdims=True) + 1e-6)).astype(BF)


def rows(n, tm):
    return pl.BlockSpec((tm, n), lambda t: (t, 0))


def when_at(step, hooks):
    for at, events in hooks.items():
        @pl.when(step == at)
        def _(events=events):
            for event in events:
                event()


def norm_phase(h, a, tm=512):
    def body(h_v, a_v):
        a_v[...] = normed(h_v[...])

    pltpu.emit_pipeline(body, grid=(T // tm,), in_specs=[rows(D, tm)], out_specs=[rows(D, tm)])(h, a)


def up_phase(a, wbuf, wait_w, act, p, q, hooks, tm=512):
    nt = T // tm

    def body(a_v, act_v, p_v, q_v):
        f, t = pl.program_id(0), pl.program_id(1)
        when_at(f * nt + t, hooks)

        @pl.when(t == 0)
        def _():
            wait_w(f)

        ra = pl.ds(pl.multiple_of(t * tm, tm), tm)
        gu = dot(a_v[ra, :], wbuf[f % 2])
        g, u = gu[:, :FT], gu[:, FT:]
        s = jax.nn.sigmoid(g)
        sl = g * s
        act_v[...] = (sl * u).astype(BF)
        p_v[...] = sl
        q_v[...] = u * (s + sl * (1 - s))

    def out():
        return pl.BlockSpec((tm, FT), lambda f, t: (t, f))

    pltpu.emit_pipeline(
        body, grid=(NF, nt), in_specs=[pl.BlockSpec((T, D), lambda f, t: (0, 0))], out_specs=[out(), out(), out()]
    )(a, act, p, q)


def down_phase(act, w, h, h1, a1, hooks, tm=256):
    def body(act_v, w_v, h_v, h1_v, a1_v):
        when_at(pl.program_id(0), hooks)
        y = dot(act_v[...], w_v[...]).astype(BF)
        total = (h_v[...].astype(F32) + y.astype(F32)).astype(BF)
        h1_v[...] = total
        a1_v[...] = normed(total)

    pltpu.emit_pipeline(
        body,
        grid=(T // tm,),
        in_specs=[rows(F, tm), pl.BlockSpec((F, D), lambda t: (0, 0)), rows(D, tm)],
        out_specs=[rows(D, tm), rows(D, tm)],
    )(act, w, h, h1, a1)


def last_phase(a, wbuf, wait_w, dy, wd, act, dgu, hooks, tm=512):
    nt = T // tm

    def body(a_v, dy_v, wd_v, act_v, d_v):
        f, t = pl.program_id(0), pl.program_id(1)
        when_at(f * nt + t, hooks)

        @pl.when(t == 0)
        def _():
            wait_w(f)

        ra = pl.ds(pl.multiple_of(t * tm, tm), tm)
        gu = dot(a_v[ra, :], wbuf[f % 2])
        g, u = gu[:, :FT], gu[:, FT:]
        s = jax.nn.sigmoid(g)
        sl = g * s
        act_v[...] = (sl * u).astype(BF)
        by = dot(dy_v[ra, :], wd_v[...], ((1,), (1,))).astype(BF).astype(F32)
        d_v[:, :FT] = (by * (u * (s + sl * (1 - s)))).astype(BF)
        d_v[:, FT:] = (by * sl).astype(BF)

    def whole():
        return pl.BlockSpec((T, D), lambda f, t: (0, 0))

    pltpu.emit_pipeline(
        body,
        grid=(NF, nt),
        in_specs=[whole(), whole(), pl.BlockSpec((FT, D), lambda f, t: (f, 0))],
        out_specs=[pl.BlockSpec((tm, FT), lambda f, t: (t, f)), pl.BlockSpec((tm, W2), lambda f, t: (t, f))],
    )(a, dy, wd, act, dgu)


def hidden_phase(dy, w, p, q, dgu, f0, f1, tm=1024):
    def body(dy_v, w_v, p_v, q_v, d_v):
        ra = pl.ds(pl.multiple_of(pl.program_id(1) * tm, tm), tm)
        by = dot(dy_v[ra, :], w_v[...], ((1,), (1,))).astype(BF).astype(F32)
        d_v[:, :FT] = (by * q_v[...]).astype(BF)
        d_v[:, FT:] = (by * p_v[...]).astype(BF)

    def tile(n):
        return pl.BlockSpec((tm, n), lambda f, t: (t, f + f0))

    pltpu.emit_pipeline(
        body,
        grid=(f1 - f0, T // tm),
        in_specs=[
            pl.BlockSpec((T, D), lambda f, t: (0, 0)),
            pl.BlockSpec((FT, D), lambda f, t: (f + f0, 0)),
            tile(FT),
            tile(FT),
        ],
        out_specs=[tile(W2)],
    )(dy, w, p, q, dgu)


def by_down_phase(act, dy, o, tf=640):
    def body(a_v, d_v, o_v):
        o_v[...] = dot(a_v[...], d_v[...], ((0,), (0,))).astype(BF)

    pltpu.emit_pipeline(
        body,
        grid=(F // tf,),
        in_specs=[pl.BlockSpec((T, tf), lambda f: (0, f)), pl.BlockSpec((T, D), lambda f: (0, 0))],
        out_specs=[pl.BlockSpec((tf, D), lambda f: (f, 0))],
    )(act, dy, o)


def by_up_phase(a, dgu, o, f0, f1):
    def body(a_v, d_v, o_v):
        o_v[...] = dot(a_v[...], d_v[...], ((0,), (0,))).astype(BF)

    pltpu.emit_pipeline(
        body,
        grid=(f1 - f0,),
        in_specs=[pl.BlockSpec((T, D), lambda f: (0, 0)), pl.BlockSpec((T, W2), lambda f: (0, f + f0))],
        out_specs=[pl.BlockSpec((D, W2), lambda f: (0, f))],
    )(a, dgu, o)


def by_h_phase(dgu, w, h, dh, o, t0, t1, tm=256):
    def body(d_v, w_v, h_v, dh_v, o_v):
        by = dot(d_v[...], w_v[...], ((1,), (1,))).astype(BF).astype(F32)
        wide = h_v[...].astype(F32)
        r = lax.rsqrt(jnp.mean(wide * wide, -1, keepdims=True) + 1e-6)
        c = jnp.sum(by * wide, -1, keepdims=True) * (r * r * r) * (1.0 / D)
        back = (by * r - wide * c).astype(BF).astype(F32)
        o_v[...] = (dh_v[...].astype(F32) + back).astype(BF)

    def tile(n):
        return pl.BlockSpec((tm, n), lambda t: (t + t0 // tm, 0))

    pltpu.emit_pipeline(
        body,
        grid=((t1 - t0) // tm,),
        in_specs=[tile(2 * F), pl.BlockSpec((D, 2 * F), lambda t: (0, 0)), tile(D), tile(D)],
        out_specs=[tile(D)],
    )(dgu, w, h, dh, o)


def add_phase(steps, ins, outs):
    n = len(ins)

    def body(*refs):
        total = refs[0][...].astype(F32)
        for ref in refs[1:n]:
            total = total + ref[...].astype(F32)
        for ref in refs[n:]:
            ref[...] = total.astype(ref.dtype)

    pltpu.emit_pipeline(
        body,
        grid=(steps,),
        in_specs=[pl.BlockSpec(shape, at) for _, shape, at in ins],
        out_specs=[pl.BlockSpec(shape, at) for _, shape, at in outs],
    )(*(ref for ref, _, _ in ins), *(ref for ref, _, _ in outs))


UNITS = ((400, D), (128, CA), (128, CB), (400, D), (128, CA), (128, CB))
NAG = 14


def unit_shapes(r, c):
    h = c // 2
    return [
        ((8 * r, c), BF),
        ((4 * r, c), BF),
        ((4 * r, h), BF),
        ((4 * r, h), BF),
        ((2 * r, h), BF),
        ((2 * r, h), BF),
        ((r, c), F32),
        ((r, c), BF),
        ((r, c), BF),
    ]


def kernel(x, dy, wgu0, wgu1, wd0, wd1, *rest):
    dx, outs = rest[0], rest[1:7]
    WGU0, WGU1, WD0, WD1, a0, h1, a1, act0, act1, p, q, dgu0, dgu1, dh1 = rest[7:21]
    bufs = [rest[21 + 9 * u : 30 + 9 * u] for u in range(6)]
    wbuf, wsem, ag_send, ag_recv, ag_loc, rs_send, rs_recv = rest[75:]

    rep, z, me = lax.axis_index("rep"), lax.axis_index("r"), lax.axis_index("s")
    mx, my, mc = me // 4, (me // 2) % 2, me % 2
    sx, sy, sc = me + 4 * (1 - 2 * mx), me + 2 * (1 - 2 * my), me + (1 - 2 * mc)
    to_x, to_y, to_c, to_z = (rep, z, sx), (rep, z, sy), (rep, z, sc), (rep, 1 - z, me)
    sf, sg = sx + z * (sy - sx), sy + z * (sx - sy)
    sd = sx + sy - me
    to_f, to_g = (rep, z, sf), (rep, z, sg)

    barrier = pltpu.get_barrier_semaphore()
    for there in (to_x, to_y, to_c, to_z):
        pl.semaphore_signal(barrier, inc=1, device_id=there, device_id_type=MESH)
    pl.semaphore_wait(barrier, 4)

    def piece(u, s):
        if u < 5 or u >= 9:
            whole, own, f = (WGU0, wgu0, u) if u < 5 else (WGU1, wgu1, u - 9)
            cols = pl.ds(f * W2, W2)
            return whole.at[pl.ds(pl.multiple_of(s * 128, 128), 128), cols], own.at[:, cols]
        whole, own = (WD0, wd0) if u < 7 else (WD1, wd1)
        cols = pl.ds((u - 5) % 2 * 512, 512)
        return whole.at[pl.ds(pl.multiple_of(s * 400, 400), 400), cols], own.at[:, cols]

    def remote(src, dst, send, recv, there):
        return pltpu.make_async_remote_copy(
            src_ref=src, dst_ref=dst, send_sem=send, recv_sem=recv, device_id=there, device_id_type=MESH
        )

    def fetch(u, k, s, own, there):
        dst, mine = piece(u, s)
        return remote(mine if own else dst, dst, ag_send.at[u, k], ag_recv.at[u, k], there)

    def fetches(u, *ks):
        plan = (
            (me, True, to_f),
            (me, True, to_c),
            (sf, False, to_z),
            (sf, False, to_g),
            (sf, False, to_c),
            (sg, False, to_c),
            (sd, False, to_c),
        )
        return [fetch(u, k, *plan[k]) for k in ks]

    def arrival(u, k, s):
        dst, _ = piece(u, s)
        return remote(dst, dst, ag_send.at[u, k], ag_recv.at[u, k], to_c)

    def local(u):
        dst, mine = piece(u, me)
        return pltpu.make_async_copy(mine, dst, ag_loc.at[u])

    def start(u):
        def event():
            local(u).start()
            for copy in fetches(u, 0, 1):
                copy.start()
        return event

    def forward(u):
        def event():
            arrival(u, 0, sf).wait_recv()
            for copy in fetches(u, 2, 3, 4):
                copy.start()
        return event

    def across(u):
        def event():
            arrival(u, 2, sg).wait_recv()
            arrival(u, 3, sd).wait_recv()
            for copy in fetches(u, 5, 6):
                copy.start()
        return event

    def here(u):
        def event():
            local(u).wait()
            other = 1 - 2 * mc
            for k, s in ((1, me), (4, sf), (5, sg), (6, sd)):
                arrival(u, k, s + other).wait_recv()
            for copy in fetches(u, *range(7)):
                copy.wait_send()
        return event

    def load(whole, f):
        return pltpu.make_async_copy(whole.at[:, pl.ds(pl.multiple_of(f * W2, W2), W2)], wbuf.at[f % 2], wsem.at[f % 2])

    def start_load(whole, f):
        return lambda: load(whole, f).start()

    def remote_rs(u, k, src, dst, there):
        return remote(src, dst, rs_send.at[u, k], rs_recv.at[u, k], there)

    def cut(ref, r, i, n=1):
        return ref.at[pl.ds(pl.multiple_of(i * r, r), n * r), :]

    def rs_copies(u, stage):
        r = UNITS[u][0]
        G, RD, SB, R1, SC, R2, VF, SV, RZ = bufs[u]
        if stage == 0:
            return [remote_rs(u, j, cut(G, r, 2 * j + 1 - mc), cut(RD, r, j), to_c) for j in range(4)]
        if stage == 1:
            return [
                remote_rs(u, 4, cut(SB, r, 0, 2), cut(R1, r, 0, 2), to_x),
                remote_rs(u, 5, cut(SB, r, 2, 2), cut(R1, r, 2, 2), to_y),
            ]
        if stage == 2:
            return [
                remote_rs(u, 6, cut(SC, r, 0), cut(R2, r, 0), to_y),
                remote_rs(u, 7, cut(SC, r, 1), cut(R2, r, 1), to_x),
            ]
        return [remote_rs(u, 8, SV, RZ, to_z)]

    def rs(u, stage):
        r, c = UNITS[u]
        h = c // 2
        G, RD, SB, R1, SC, R2, VF, SV, RZ = bufs[u]
        if stage > 0:
            for copy in rs_copies(u, stage - 1):
                copy.wait()
        half = (r, h)
        own = 2 * mx + my
        if stage == 1:
            def chip(i):
                cx = (1 - mx) + (i // 2) * (1 - i % 2) * (2 * mx - 1)
                cy = my + ((i + 3) // 4) * (1 - 2 * my)
                return 2 * cx + cy
            add_phase(
                4,
                [(G, half, lambda i: (2 * chip(i) + mc, i // 2)), (RD, half, lambda i: (chip(i), i // 2))],
                [(SB, half, lambda i: (i, 0))],
            )
        if stage == 2:
            def chip(i):
                return 2 * (mx + i * (1 - 2 * mx)) + my + (1 - i) * (1 - 2 * my)
            add_phase(
                2,
                [
                    (G, half, lambda i: (2 * chip(i) + mc, i)),
                    (RD, half, lambda i: (chip(i), i)),
                    (R1, half, lambda i: (1 + 2 * i, 0)),
                ],
                [(SC, half, lambda i: (i, 0))],
            )
        if stage == 3:
            add_phase(
                2,
                [
                    (G, half, lambda i: (2 * own + mc, i)),
                    (RD, half, lambda i: (own, i)),
                    (R1, half, lambda i: (2 * i, 0)),
                    (R2, half, lambda i: (i, 0)),
                ],
                [(VF, half, lambda i: (0, i)), (SV, half, lambda i: (0, i))],
            )
        if stage == 4:
            add_phase(
                2,
                [(VF, half, lambda i: (0, i)), (RZ, half, lambda i: (0, i))],
                [(outs[u], half, lambda i: (0, i))],
            )
            return
        for copy in rs_copies(u, stage):
            copy.start()

    for u in range(3):
        start(u)()
    norm_phase(x, a0)
    for event in (forward(0), start(3), across(0), forward(1), start(4), here(0), start_load(WGU0, 0)):
        event()
    hooks = {}
    for f in range(5):
        events = hooks.setdefault(4 * f, [])
        events.append(forward(f + 2))
        events.append(start(f + 5))
        hooks[4 * f + 1] = [across(f + 1)]
        hooks[4 * f + 2] = [here(f + 1)]
        if f < 4:
            hooks[4 * f + 2].append(start_load(WGU0, f + 1))
    up_phase(a0, wbuf, lambda f: load(WGU0, f).wait(), act0, p, q, hooks)
    for event in (across(6), forward(7), start(10), here(6)):
        event()
    down_phase(
        act0,
        WD0,
        x,
        h1,
        a1,
        {2: [across(7), forward(8), start(11)], 4: [here(7), across(8), forward(9), start(12)], 6: [here(8), across(9), forward(10), start(13)]},
    )
    for event in (here(9), start_load(WGU1, 0)):
        event()
    hooks = {}
    for f in range(4):
        hooks[4 * f] = [across(f + 10)] + ([forward(f + 11)] if f < 3 else [])
        hooks[4 * f + 2] = [here(f + 10), start_load(WGU1, f + 1)]
    last_phase(a1, wbuf, lambda f: load(WGU1, f).wait(), dy, WD1, act1, dgu1, hooks)

    G = [b[0] for b in bufs]
    by_down_phase(act1, dy, G[0])
    rs(0, 0)
    by_up_phase(a1, dgu1, G[1], 0, 3)
    rs(0, 1)
    rs(1, 0)
    by_up_phase(a1, dgu1, G[2], 3, 5)
    rs(0, 2)
    rs(1, 1)
    rs(2, 0)
    by_h_phase(dgu1, WGU1, h1, dy, dh1, 0, T // 2)
    rs(0, 3)
    rs(1, 2)
    rs(2, 1)
    by_h_phase(dgu1, WGU1, h1, dy, dh1, T // 2, T)
    rs(1, 3)
    by_down_phase(act0, dh1, G[3])
    rs(3, 0)
    rs(2, 2)
    rs(0, 4)
    hidden_phase(dh1, WD0, p, q, dgu0, 0, 3)
    rs(3, 1)
    rs(2, 3)
    rs(1, 4)
    by_up_phase(a0, dgu0, G[4], 0, 3)
    rs(4, 0)
    rs(3, 2)
    hidden_phase(dh1, WD0, p, q, dgu0, 3, 5)
    rs(4, 1)
    rs(3, 3)
    rs(2, 4)
    by_up_phase(a0, dgu0, G[5], 3, 5)
    rs(5, 0)
    by_h_phase(dgu0, WGU0, x, dh1, dx, 0, T // 4)
    rs(5, 1)
    rs(4, 2)
    by_h_phase(dgu0, WGU0, x, dh1, dx, T // 4, T)
    rs(3, 4)
    rs(4, 3)
    rs(5, 2)
    rs(5, 3)
    rs(4, 4)
    rs(5, 4)


def solution(mesh):
    def step(x, dy, w_gate, w_up, w_down):
        def tiles(g, u):
            both = jnp.stack([g.reshape(128, NF, FT), u.reshape(128, NF, FT)], 2)
            return both.reshape(128, 2 * F)

        shapes = [((T, D), BF)]
        shapes += [(s, BF) for s in UNITS]
        shapes += [((D, 2 * F), BF)] * 2 + [((F, D), BF)] * 2 + [((T, D), BF)] * 3
        shapes += [((T, F), BF)] * 2 + [((T, F), F32)] * 2 + [((T, 2 * F), BF)] * 2 + [((T, D), BF)]
        for unit in UNITS:
            shapes += unit_shapes(*unit)
        anywhere = pl.BlockSpec(memory_space=pl.ANY)
        flops = 17 * 2 * T * D * F
        res = pl.pallas_call(
            kernel,
            out_shape=[jax.ShapeDtypeStruct(s, t) for s, t in shapes],
            in_specs=[anywhere] * 6,
            out_specs=[anywhere] * len(shapes),
            scratch_shapes=[
                pltpu.VMEM((2, D, W2), BF),
                pltpu.SemaphoreType.DMA((2,)),
                pltpu.SemaphoreType.DMA((NAG, 7)),
                pltpu.SemaphoreType.DMA((NAG, 7)),
                pltpu.SemaphoreType.DMA((NAG,)),
                pltpu.SemaphoreType.DMA((6, 9)),
                pltpu.SemaphoreType.DMA((6, 9)),
            ],
            compiler_params=pltpu.CompilerParams(
                collective_id=0, has_side_effects=True, vmem_limit_bytes=62 * 2**20
            ),
            cost_estimate=pl.CostEstimate(flops=flops, bytes_accessed=2**30, transcendentals=0),
            name="step",
        )(x[0], dy[0], tiles(w_gate[0], w_up[0]), tiles(w_gate[1], w_up[1]), w_down[0], w_down[1])
        dx, gd1, ga1, gb1, gd0, ga0, gb0 = res[:7]

        def untiled(a, b, i):
            return jnp.concatenate([v.reshape(128, -1, 2, FT)[:, :, i].reshape(128, -1) for v in (a, b)], -1)

        gates, ups = (jnp.stack([untiled(ga0, gb0, i), untiled(ga1, gb1, i)]) for i in range(2))
        return dx[None], gates, ups, jnp.stack([gd0, gd1])

    states, cut = P(("rep", "r", "s"), None, None), P(None, "s", None)
    return jax.shard_map(
        step,
        mesh=mesh,
        in_specs=(states, states) + (cut,) * 3,
        out_specs=(states,) + (P("rep", "s", None),) * 3,
        check_vma=False,
    )
```

time: 889 us -> 606 us (0.68)
  Pallas kernels: 0 us -> 540 us
  matrix products: 422 us -> 0 us
  waiting for transfers between devices: 396 us -> 0 us
  local copies, waits for them, and re-layouts: 28.7 us -> 50.7 us
  other arithmetic: 19.4 us -> 3.2 us
  between operations: 14.5 us -> 1.32 us
    pallas_call x0 -> x1, Pallas kernels: none -> 540 us  [step(): pl.pallas_call(kernel, out_shape=[jax.ShapeDtypeStruct(s, t) for s, t in...]
    dot_general x17 -> x0, matrix products: 422 us -> none  [the longest x6 149 us: layer(): up = jnp.dot(a, w['w_up'], preferred_element_type=jnp.float32)]
    reduce_scatter x6 -> x0, waiting for transfers between devices: 200 us -> none  [summed(): lax.psum_scatter(term, 's', scatter_dimension=0, tiled=True)]
    all_gather x6 -> x0, waiting for transfers between devices: 125 us -> none  [fetched(): lax.all_gather(w[number], 's', axis=0, tiled=True)]
    psum x1 -> x0, waiting for transfers between devices: 68.9 us -> none  [summed(): lax.psum(lax.psum_scatter(term, 's', scatter_dimension=0, tiled=True), 'r')]
    unnamed x33 -> x35, local copies, waits for them, and re-layouts: 21.9 us -> 23.9 us
  transfers between devices with their start and end apart: 13 -> 0, of which waited for: 11 -> 0; matrix products, arithmetic and copies ran while one was open for 40% -> 0% of each run, Pallas kernels for 0% -> 0%
where the time goes in v1:
time: 606 us; the launch traced here: 596 us
  Pallas kernels  540 us (89%)
  local copies, waits for them, and re-layouts  50.7 us (8%)
    pallas_call x1, Pallas kernels, step(): pl.pallas_call(kernel, out_shape=[jax.ShapeDtypeStruct(s, t) for s, t in...  540 us
    unnamed x35, local copies, waits for them, and re-layouts  23.9 us

profile of v1, /device:TPU:0, one launch (start us, length us, event | category | flops | bytes accessed | tf_op | source)
XLA Modules:
  0.0 595.5 jit_solution(3160081816389738295)
XLA Ops:
  0.6 1.5 fusion
  2.1 0.8 copy.31
  3.0 1.3 copy.29
  4.3 2.4 fusion.1
  6.7 0.8 copy.32
  7.5 0.2 pad_maximum_fusion.1
  7.6 3.7 copy.18
  11.4 0.0 copy-start.1
  11.4 2.0 reshape.31.wgu1
  13.4 0.0 copy-done.1
  13.4 0.8 copy.30
  14.2 0.3 copy-done
  14.5 0.2 pad_maximum_fusion
  14.7 3.7 copy.15
  18.4 0.0 copy-start.3
  18.4 2.0 reshape.30.wgu0
  20.4 0.0 copy-done.3
  20.4 1.3 slice_bitcast_fusion
  21.7 540.3 %step.1 = (bf16[2048,1024]{1,0:T(8,128)(2,1)}, bf16[400,1024]{1,0:T(8,128)(2,1)}, bf16[128,3840]{1,0:T(8,128)(2,1)}, bf16[128,2560]{1,0:T(8,128)(2,1)}, bf16[400...) custom-call(bf16[2048,1024]{1,0:T(8,128)(2,1)} %bitcast.44, ...), custom_call_target="tpu_custom_call" | custom-call | flops 228170137600 | bytes 1073741824 | tf_op jit(solution)/shard_map/step/pallas_call | solution.py:486
  562.0 2.1 reshape.33
  564.2 0.2 reshape.35
  564.3 0.9 fusion.5
  565.3 1.1 copy.40
  566.4 1.1 copy.36
  567.5 0.9 fusion.4
  568.4 1.1 copy.38
  569.5 1.1 copy.34
  570.6 0.2 reshape.32
  570.9 2.3 reshape.34
  573.2 2.2 fusion.3
  575.4 3.0 copy.39
  578.4 0.7 copy.35
  579.1 1.4 fusion.2
  580.5 0.0 copy-start.2
  580.5 0.7 copy.37
  581.3 0.3 copy-done.2
  581.5 1.2 maximum_bitcast_fusion.2
  582.7 0.2 pad_maximum_fusion.3
  582.9 0.0 copy-start.4
  582.9 2.5 copy.28
  585.4 0.7 copy.33
  586.1 0.2 copy-done.5
  586.4 0.1 maximum_bitcast_fusion
  586.5 0.2 pad_maximum_fusion.2
  586.7 2.5 copy.27
  589.1 0.0 copy-done.8
  589.1 1.3 pad_maximum_fusion.4
  590.5 4.6 copy.42
  (10 shorter events, 0.0 us)
Async XLA Ops:
  11.4 2.0 copy-start.1
  13.4 1.1 copy-start
  18.4 2.0 copy-start.3
  562.0 2.1 copy-start.9
  568.4 2.2 copy-start.6
  580.5 1.0 copy-start.2
  582.9 3.2 copy-start.4
  585.4 1.0 copy-start.5
  586.6 2.5 copy-start.7
  586.6 2.5 copy-start.8

commit v2 on v0

v2 whole, which is shorter than its diff:
```python
import jax
import jax.numpy as jnp
from jax import lax
from jax.experimental import pallas as pl
from jax.experimental.pallas import tpu as pltpu
from jax.sharding import PartitionSpec as P

BF, F32 = jnp.bfloat16, jnp.float32
MESH = pl.DeviceIdType.MESH
T, D, F = 2048, 1024, 3200
FT, NF = 640, 5
W2 = 2 * FT
CA, CB = 3 * W2, 2 * W2


NT, TN = ((1,), (1,)), ((0,), (0,))


def dot(a, b, contract=((1,), (0,))):
    return lax.dot_general(a, b, (contract, ((), ())), preferred_element_type=F32)


def normed(h):
    wide = h.astype(F32)
    return (wide * lax.rsqrt(jnp.mean(wide * wide, -1, keepdims=True) + 1e-6)).astype(BF)


def rows(n, tm):
    return pl.BlockSpec((tm, n), lambda t: (t, 0))


def origin(*_):
    return 0, 0


def when_at(step, hooks):
    for at, events in hooks.items():
        @pl.when(step == at)
        def _(events=events):
            for event in events:
                event()


def norm_phase(h, a, tm=256):
    def body(h_v, a_v):
        a_v[...] = normed(h_v[...])

    pltpu.emit_pipeline(body, grid=(T // tm,), in_specs=[rows(D, tm)], out_specs=[rows(D, tm)])(h, a)


def run(body, grid, ins, outs, sides=()):
    ins, outs = list(ins), list(outs)
    m, n = len(ins), len(outs)

    def at(steps, index):
        def block(*g):
            flat = g[0] if len(g) == 1 else g[0] * grid[1] + g[1]
            return index(jnp.minimum(flat, steps - 1))
        return block

    for steps, more, results in sides:
        ins += [(ref, shape, at(steps, index)) for ref, shape, index in more]
    for steps, more, results in sides:
        outs += [(ref, shape, at(steps, index)) for ref, shape, index in results]

    def whole(*refs):
        mains, side_ins = refs[:m], refs[m : len(ins)]
        results, side_outs = refs[len(ins) : len(ins) + n], refs[len(ins) + n :]
        body(*mains, *results)
        for _, more, sums in sides:
            total = side_ins[0][...].astype(F32)
            for ref in side_ins[1 : len(more)]:
                total = total + ref[...].astype(F32)
            for ref in side_outs[: len(sums)]:
                ref[...] = total.astype(ref.dtype)
            side_ins, side_outs = side_ins[len(more) :], side_outs[len(sums) :]

    pltpu.emit_pipeline(
        whole,
        grid=grid,
        in_specs=[pl.BlockSpec(shape, index) for _, shape, index in ins],
        out_specs=[pl.BlockSpec(shape, index) for _, shape, index in outs],
    )(*(ref for ref, _, _ in ins), *(ref for ref, _, _ in outs))


def add_phase(steps, ins, outs):
    run(lambda *refs: None, (steps,), [], [], [(steps, ins, outs)])


def join_phase(g, u, whole, me):
    def body(g_v, u_v, o_v):
        o_v[:, :FT] = g_v[...]
        o_v[:, FT:] = u_v[...]

    run(
        body,
        (NF,),
        [(g, (RU, FT), lambda f: (0, f)), (u, (RU, FT), lambda f: (0, f))],
        [(whole, (RU, W2), lambda f: (me, f))],
    )


def copy_phase(w, whole, me):
    def body(w_v, o_v):
        o_v[...] = w_v[...]

    run(body, (2,), [(w, (RD_, D // 2), lambda i: (0, i))], [(whole, (RD_, D // 2), lambda i: (me, i))])


def gated(gu):
    g, u = gu[:, :FT], gu[:, FT:]
    s = jax.nn.sigmoid(g)
    sl = g * s
    return sl, u * (s + sl * (1 - s)), sl * u


def up_phase(a, wbuf, wait_w, act, p, q, hooks, tm=1024, sub=512):
    nt, ns = T // tm, tm // sub

    def body(a_v, act_v, p_v, q_v):
        f, t = pl.program_id(0), pl.program_id(1)

        @pl.loop(0, ns)
        def _(i):
            piece = t * ns + i
            when_at(f * nt * ns + piece, hooks)

            @pl.when(piece == 0)
            def _():
                wait_w(f)

            ra, r = (pl.ds(pl.multiple_of(j * sub, sub), sub) for j in (piece, i))
            p_v[r, :], q_v[r, :], hidden = gated(dot(a_v[ra, :], wbuf[f % 2]))
            act_v[r, :] = hidden.astype(BF)

    def tile(ref):
        return ref, (tm, FT), lambda f, t: (t, f)

    run(body, (NF, nt), [(a, (T, D), origin)], [tile(act), tile(p), tile(q)])


def down_phase(act, w, h, h1, a1, hooks, tm=256):
    def body(act_v, w_v, h_v, h1_v, a1_v):
        when_at(pl.program_id(0), hooks)
        y = dot(act_v[...], w_v[...]).astype(BF)
        total = (h_v[...].astype(F32) + y.astype(F32)).astype(BF)
        h1_v[...] = total
        a1_v[...] = normed(total)

    def tile(ref, n=D):
        return ref, (tm, n), lambda t: (t, 0)

    run(body, (T // tm,), [tile(act, F), (w, (F, D), origin), tile(h)], [tile(h1), tile(a1)])


def last_phase(a, wbuf, wait_w, dy, wd, dgu, o, acc, hooks, tm=1024, sub=512):
    nt, ns = T // tm, tm // sub

    def body(a_v, dy_v, wd_v, d_v, o_v):
        f, t = pl.program_id(0), pl.program_id(1)

        @pl.loop(0, ns)
        def _(i):
            piece = t * ns + i
            when_at(f * nt * ns + piece, hooks)

            @pl.when(piece == 0)
            def _():
                wait_w(f)

            ra, r = (pl.ds(pl.multiple_of(j * sub, sub), sub) for j in (piece, i))
            p, q, hidden = gated(dot(a_v[ra, :], wbuf[f % 2]))
            by = dot(dy_v[ra, :], wd_v[...], NT).astype(BF).astype(F32)
            d_v[r, :FT] = (by * q).astype(BF)
            d_v[r, FT:] = (by * p).astype(BF)
            term = dot(hidden.astype(BF), dy_v[ra, :], TN)

            @pl.when(piece == 0)
            def _():
                acc[:FT, :] = term

            @pl.when(piece > 0)
            def _():
                acc[:FT, :] += term

        @pl.when(t == nt - 1)
        def _():
            o_v[...] = acc[:FT, :].astype(BF)

    run(
        body,
        (NF, nt),
        [(a, (T, D), origin), (dy, (T, D), origin), (wd, (FT, D), lambda f, t: (f, 0))],
        [(dgu, (tm, W2), lambda f, t: (t, f)), (o, (FT, D), lambda f, t: (f, 0))],
    )


def hidden_phase(dy, w, act, p, q, dgu, o, acc, f0, f1, sides=(), tm=1024):
    nt = T // tm

    def body(dy_v, w_v, act_v, p_v, q_v, d_v, o_v):
        t = pl.program_id(1)
        ra = pl.ds(pl.multiple_of(t * tm, tm), tm)
        by = dot(dy_v[ra, :], w_v[...], NT).astype(BF).astype(F32)
        d_v[:, :FT] = (by * q_v[...]).astype(BF)
        d_v[:, FT:] = (by * p_v[...]).astype(BF)
        term = dot(act_v[...], dy_v[ra, :], TN)

        @pl.when(t == 0)
        def _():
            acc[:FT, :] = term

        @pl.when(t == nt - 1)
        def _():
            o_v[...] = (acc[:FT, :] + term).astype(BF)

    def tile(ref, n):
        return ref, (tm, n), lambda f, t: (t, f + f0)

    def row(ref):
        return ref, (FT, D), lambda f, t: (f + f0, 0)

    run(
        body,
        (f1 - f0, nt),
        [(dy, (T, D), origin), row(w), tile(act, FT), tile(p, FT), tile(q, FT)],
        [tile(dgu, W2), row(o)],
        sides,
    )


def by_up_phase(a, dgu, o, f0, f1, sides=(), hooks={}, sub=512):
    def body(a_v, d_v, o_v):
        when_at(pl.program_id(0), hooks)

        @pl.loop(0, D // sub)
        def _(i):
            r = pl.ds(pl.multiple_of(i * sub, sub), sub)
            o_v[r, :] = dot(a_v[:, r], d_v[...], TN).astype(BF)

    run(
        body,
        (f1 - f0,),
        [(a, (T, D), origin), (dgu, (T, W2), lambda f: (0, f + f0))],
        [(o, (D, W2), lambda f: (0, f))],
        sides,
    )


def by_h_phase(dgu, w, acc, k0, k1, sides=(), hooks={}, sub=1024):
    def body(d_v, w_v):
        when_at(pl.program_id(0), hooks)
        if k0 == 0:
            @pl.when(pl.program_id(0) == 0)
            def _():
                acc[...] = jnp.zeros_like(acc)

        @pl.loop(0, T // sub)
        def _(i):
            r = pl.ds(pl.multiple_of(i * sub, sub), sub)
            acc[r, :] += dot(d_v[r, :], w_v[...], NT)

    run(
        body,
        (k1 - k0,),
        [(dgu, (T, W2), lambda k: (0, k + k0)), (w, (D, W2), lambda k: (0, k + k0))],
        [],
        sides,
    )


def by_h_end(acc, h, dh, o, tm=256):
    def body(h_v, dh_v, o_v):
        by = acc[pl.ds(pl.multiple_of(pl.program_id(0) * tm, tm), tm), :].astype(BF).astype(F32)
        wide = h_v[...].astype(F32)
        r = lax.rsqrt(jnp.mean(wide * wide, -1, keepdims=True) + 1e-6)
        c = jnp.sum(by * wide, -1, keepdims=True) * (r * r * r) * (1.0 / D)
        back = (by * r - wide * c).astype(BF).astype(F32)
        o_v[...] = (dh_v[...].astype(F32) + back).astype(BF)

    def tile(ref):
        return ref, (tm, D), lambda t: (t, 0)

    run(body, (T // tm,), [tile(h), tile(dh)], [tile(o)])


RU, RD_ = D // 8, F // 8
D1, A1, B1, D0, A0, B0 = range(6)
CORE, NEAR, FAR, GROUP = range(4)
UNITS = 2 * ((RD_, D), (RU, CA), (RU, CB))
NAG = 14


def unit_shapes(r, c):
    h = c // 2
    return [
        ((8 * r, c), BF),
        ((4 * r, c), BF),
        ((4 * r, h), BF),
        ((4 * r, h), BF),
        ((2 * r, h), BF),
        ((2 * r, h), BF),
        ((r, c), F32),
        ((r, c), BF),
        ((r, c), BF),
    ]


def kernel(x, dy, w_gate, w_up, w_down, dx, *rest):
    x, dy = x.at[0], dy.at[0]
    WGU0, WGU1, WD0, WD1, a0, h1, a1, act0, p, q, dgu0, dgu1, dh1 = rest[:13]
    bufs = [rest[13 + 9 * u :][:9] for u in range(len(UNITS))]
    wbuf, acc, wsem, ag_send, ag_recv, rs_send, rs_recv = rest[13 + 9 * len(UNITS) :]

    rep, z, me = lax.axis_index("rep"), lax.axis_index("r"), lax.axis_index("s")
    mx, my, mc = me // 4, (me // 2) % 2, me % 2
    sx, sy, sc = me + 4 * (1 - 2 * mx), me + 2 * (1 - 2 * my), me + (1 - 2 * mc)
    to_x, to_y, to_c, to_z = (rep, z, sx), (rep, z, sy), (rep, z, sc), (rep, 1 - z, me)
    sf, sg = sx + z * (sy - sx), sy + z * (sx - sy)
    sd = sx + sy - me
    to_f, to_g = (rep, z, sf), (rep, z, sg)

    barrier = pltpu.get_barrier_semaphore()
    for there in (to_x, to_y, to_c, to_z):
        pl.semaphore_signal(barrier, inc=1, device_id=there, device_id_type=MESH)
    pl.semaphore_wait(barrier, 4)

    def piece(u, s):
        if u < 5 or u >= 9:
            whole, f = (WGU0, u) if u < 5 else (WGU1, u - 9)
            return whole.at[pl.ds(pl.multiple_of(s * RU, RU), RU), pl.ds(f * W2, W2)]
        whole = WD0 if u < 7 else WD1
        return whole.at[pl.ds(pl.multiple_of(s * RD_, RD_), RD_), pl.ds((u - 5) % 2 * 512, 512)]

    def remote(src, dst, send, recv, there):
        return pltpu.make_async_remote_copy(
            src_ref=src, dst_ref=dst, send_sem=send, recv_sem=recv, device_id=there, device_id_type=MESH
        )

    def fetches(u, *ks):
        plan = ((me, to_f), (me, to_c), (sf, to_z), (sf, to_g), (sf, to_c), (sg, to_c), (sd, to_c))
        return [
            remote(piece(u, plan[k][0]), piece(u, plan[k][0]), ag_send.at[u, k], ag_recv.at[u, k], plan[k][1]) for k in ks
        ]

    def arrival(u, k, s):
        return remote(piece(u, s), piece(u, s), ag_send.at[u, k], ag_recv.at[u, k], to_c)

    def start(u):
        def event():
            for copy in fetches(u, 0, 1):
                copy.start()
        return event

    def forward(u):
        def event():
            arrival(u, 0, sf).wait_recv()
            for copy in fetches(u, 2, 3, 4):
                copy.start()
        return event

    def across(u):
        def event():
            arrival(u, 2, sg).wait_recv()
            arrival(u, 3, sd).wait_recv()
            for copy in fetches(u, 5, 6):
                copy.start()
        return event

    def here(u):
        def event():
            other = 1 - 2 * mc
            for k, s in ((1, me), (4, sf), (5, sg), (6, sd)):
                arrival(u, k, s + other).wait_recv()
            for copy in fetches(u, *range(7)):
                copy.wait_send()
        return event

    def load(whole, f):
        return pltpu.make_async_copy(whole.at[:, pl.ds(pl.multiple_of(f * W2, W2), W2)], wbuf.at[f % 2], wsem.at[f % 2])

    def start_load(whole, f):
        return lambda: load(whole, f).start()

    def remote_rs(u, k, src, dst, there):
        return remote(src, dst, rs_send.at[u, k], rs_recv.at[u, k], there)

    def cut(ref, r, i, n=1):
        return ref.at[pl.ds(pl.multiple_of(i * r, r), n * r), :]

    def rs_copies(u, stage):
        r = UNITS[u][0]
        G, RD, SB, R1, SC, R2, VF, SV, RZ = bufs[u]
        if stage == 0:
            return [remote_rs(u, j, cut(G, r, 2 * j + 1 - mc), cut(RD, r, j), to_c) for j in range(4)]
        if stage == 1:
            return [
                remote_rs(u, 4, cut(SB, r, 0, 2), cut(R1, r, 0, 2), to_x),
                remote_rs(u, 5, cut(SB, r, 2, 2), cut(R1, r, 2, 2), to_y),
            ]
        if stage == 2:
            return [
                remote_rs(u, 6, cut(SC, r, 0), cut(R2, r, 0), to_y),
                remote_rs(u, 7, cut(SC, r, 1), cut(R2, r, 1), to_x),
            ]
        return [remote_rs(u, 8, SV, RZ, to_z)]

    def sums(u, stage):
        r, c = UNITS[u]
        half = (r, c // 2)
        G, RD, SB, R1, SC, R2, VF, SV, RZ = bufs[u]
        own = 2 * mx + my
        if stage == 1:
            def side(axis):
                def chip(i):
                    cx = (1 - mx) + axis * (1 - i) * (2 * mx - 1)
                    cy = my + (1 - (1 - axis) * (1 - i)) * (1 - 2 * my)
                    return 2 * cx + cy
                return (
                    2,
                    [(G, half, lambda i: (2 * chip(i) + mc, axis)), (RD, half, lambda i: (chip(i), axis))],
                    [(SB, half, lambda i: (i + 2 * axis, 0))],
                )
            return [side(0), side(1)]
        if stage == 2:
            def chip(i):
                return 2 * (mx + i * (1 - 2 * mx)) + my + (1 - i) * (1 - 2 * my)
            return [(
                2,
                [
                    (G, half, lambda i: (2 * chip(i) + mc, i)),
                    (RD, half, lambda i: (chip(i), i)),
                    (R1, half, lambda i: (1 + 2 * i, 0)),
                ],
                [(SC, half, lambda i: (i, 0))],
            )]
        return [(
            2,
            [
                (G, half, lambda i: (2 * own + mc, i)),
                (RD, half, lambda i: (own, i)),
                (R1, half, lambda i: (2 * i, 0)),
                (R2, half, lambda i: (i, 0)),
            ],
            [(VF, half, lambda i: (0, i)), (SV, half, lambda i: (0, i))],
        )]

    def send(u, stage):
        for copy in rs_copies(u, stage):
            copy.start()

    def wait(u, stage):
        for copy in rs_copies(u, stage):
            copy.wait()

    def rs(u, stage):
        wait(u, stage - 1)
        run(lambda *refs: None, (2,), [], [], sums(u, stage))
        send(u, stage)

    join_phase(w_gate.at[0], w_up.at[0], WGU0, me)
    for u in range(3):
        start(u)()
    norm_phase(x, a0)
    forward(0)()
    start(3)()
    copy_phase(w_down.at[0], WD0, me)
    copy_phase(w_down.at[1], WD1, me)
    forward(1)()
    start(4)()
    join_phase(w_gate.at[1], w_up.at[1], WGU1, me)
    for event in (across(0), here(0), start_load(WGU0, 0)):
        event()
    hooks = {}
    for f in range(5):
        events = hooks.setdefault(4 * f, [])
        events.append(forward(f + 2))
        events.append(start(f + 5))
        hooks[4 * f + 1] = [across(f + 1)]
        hooks[4 * f + 2] = [here(f + 1)]
        if f < 4:
            hooks[4 * f + 2].append(start_load(WGU0, f + 1))
    up_phase(a0, wbuf, lambda f: load(WGU0, f).wait(), act0, p, q, hooks)
    for event in (across(6), forward(7), start(10), here(6)):
        event()
    down_phase(
        act0,
        WD0,
        x,
        h1,
        a1,
        {2: [across(7), forward(8), start(11)], 4: [here(7), across(8), forward(9), start(12)], 6: [here(8), across(9), forward(10), start(13)]},
    )
    for event in (here(9), start_load(WGU1, 0)):
        event()
    hooks = {}
    for f in range(4):
        hooks[4 * f] = [across(f + 10)] + ([forward(f + 11)] if f < 3 else [])
        hooks[4 * f + 2] = [here(f + 10), start_load(WGU1, f + 1)]
    G = [b[0] for b in bufs]
    last_phase(a1, wbuf, lambda f: load(WGU1, f).wait(), dy, WD1, dgu1, G[0], acc, hooks)

    def at_once(u, stage):
        return lambda: rs(u, stage)

    send(D1, CORE)
    by_up_phase(a1, dgu1, G[A1], 0, 3)
    send(A1, CORE)
    wait(D1, CORE)
    by_up_phase(a1, dgu1, G[B1], 3, 5, sums(D1, NEAR))
    send(D1, NEAR)
    send(B1, CORE)
    wait(A1, CORE)
    by_h_phase(dgu1, WGU1, acc, 0, 3, sums(A1, NEAR))
    send(A1, NEAR)
    wait(B1, CORE)
    wait(D1, NEAR)
    by_h_phase(dgu1, WGU1, acc, 3, 5, sums(B1, NEAR) + sums(D1, FAR))
    send(D1, FAR)
    send(B1, NEAR)
    by_h_end(acc, h1, dy, dh1)
    wait(A1, NEAR)
    hidden_phase(dh1, WD0, act0, p, q, dgu0, G[D0], acc, 0, 3, sums(A1, FAR))
    send(A1, FAR)
    wait(D1, FAR)
    wait(B1, NEAR)
    hidden_phase(dh1, WD0, act0, p, q, dgu0, G[D0], acc, 3, 5, sums(D1, GROUP) + sums(B1, FAR))
    send(D0, CORE)
    send(B1, FAR)
    send(D1, GROUP)
    wait(A1, FAR)
    by_up_phase(a0, dgu0, G[A0], 0, 3, sums(A1, GROUP), {1: [at_once(D0, NEAR)]})
    send(A0, CORE)
    send(A1, GROUP)
    wait(B1, FAR)
    by_up_phase(a0, dgu0, G[B0], 3, 5, sums(B1, GROUP), {1: [at_once(D0, FAR), at_once(A0, NEAR)]})
    send(B0, CORE)
    send(B1, GROUP)
    late = {1: [at_once(D0, GROUP)], 2: [at_once(A0, FAR), at_once(B0, NEAR)], 4: [at_once(A0, GROUP)]}
    by_h_phase(dgu0, WGU0, acc, 0, NF, (), late)
    rs(B0, FAR)
    by_h_end(acc, x, dh1, dx)
    rs(B0, GROUP)
    for u in range(len(UNITS)):
        wait(u, GROUP)


def finish(dx, *refs):
    parts, (dx_o, gate_o, up_o, down_o) = refs[:12], refs[12:]

    def body(dx_v, *vs):
        ins, (dx_w, *outs) = vs[:12], vs[12:]
        i = pl.program_id(0)
        dx_w[...] = dx_v[...]
        for layer, u in ((1, 0), (0, 3)):
            d, da, db = (ins[2 * (u + k) : 2 * (u + k) + 2] for k in range(3))
            gate_w, up_w, down_w = outs[3 * layer : 3 * layer + 3]
            down_w[...] = (d[0][...] + d[1][...].astype(F32)).astype(BF)
            for use, pair in ((i < 3, da), (i >= 3, db)):
                @pl.when(use)
                def _(pair=pair, gate_w=gate_w, up_w=up_w):
                    total = (pair[0][...] + pair[1][...].astype(F32)).astype(BF)
                    gate_w[...] = total[:, :FT]
                    up_w[...] = total[:, FT:]

    def cap(i):
        return jnp.minimum(i, 3)

    ins = [(dx, (512, D), lambda i: (cap(i), 0))]
    for u in range(6):
        shape = (RD_, D // 4) if u % 3 == 0 else (RU, W2)
        index = (
            (lambda i: (0, cap(i))),
            (lambda i: (0, jnp.minimum(i, 2))),
            (lambda i: (0, jnp.maximum(i - 3, 0))),
        )[u % 3]
        ins += [(parts[2 * u], shape, index), (parts[2 * u + 1], shape, index)]
    outs = [(dx_o.at[0], (512, D), lambda i: (cap(i), 0))]
    for layer in range(2):
        outs += [
            (gate_o.at[layer], (RU, FT), lambda i: (0, i)),
            (up_o.at[layer], (RU, FT), lambda i: (0, i)),
            (down_o.at[layer], (RD_, D // 4), lambda i: (0, cap(i))),
        ]
    run(body, (NF,), ins, outs)


def solution(mesh):
    def step(x, dy, w_gate, w_up, w_down):
        shapes = [((T, D), BF)]
        shapes += [((D, 2 * F), BF)] * 2 + [((F, D), BF)] * 2 + [((T, D), BF)] * 3
        shapes += [((T, F), BF)] + [((T, F), F32)] * 2 + [((T, 2 * F), BF)] * 2 + [((T, D), BF)]
        for unit in UNITS:
            shapes += unit_shapes(*unit)
        anywhere = pl.BlockSpec(memory_space=pl.ANY)

        def arrays(shapes):
            return [jax.ShapeDtypeStruct(s, t) for s, t in shapes]

        res = pl.pallas_call(
            kernel,
            out_shape=arrays(shapes),
            in_specs=[anywhere] * 5,
            out_specs=[anywhere] * len(shapes),
            scratch_shapes=[
                pltpu.VMEM((2, D, W2), BF),
                pltpu.VMEM((T, D), F32),
                pltpu.SemaphoreType.DMA((2,)),
                pltpu.SemaphoreType.DMA((NAG, 7)),
                pltpu.SemaphoreType.DMA((NAG, 7)),
                pltpu.SemaphoreType.DMA((6, 9)),
                pltpu.SemaphoreType.DMA((6, 9)),
            ],
            compiler_params=pltpu.CompilerParams(
                collective_id=0, has_side_effects=True, vmem_limit_bytes=62 * 2**20
            ),
            cost_estimate=pl.CostEstimate(flops=17 * 2 * T * D * F, bytes_accessed=2**30, transcendentals=0),
            name="step",
        )(x, dy, w_gate, w_up, w_down)
        last = [res[14 + 9 * u + k] for u in range(len(UNITS)) for k in (6, 8)]
        outs = [((1, T, D), BF), ((2, RU, F), BF), ((2, RU, F), BF), ((2, RD_, D), BF)]
        return pl.pallas_call(
            finish,
            out_shape=arrays(outs),
            in_specs=[anywhere] * 13,
            out_specs=[anywhere] * 4,
            compiler_params=pltpu.CompilerParams(vmem_limit_bytes=62 * 2**20),
            name="finish",
        )(res[0], *last)

    states, cut = P(("rep", "r", "s"), None, None), P(None, "s", None)
    return jax.shard_map(
        step,
        mesh=mesh,
        in_specs=(states, states) + (cut,) * 3,
        out_specs=(states,) + (P("rep", "s", None),) * 3,
        check_vma=False,
    )
```

time: 889 us -> 506 us (0.57)
  Pallas kernels: 0 us -> 504 us
  matrix products: 422 us -> 0 us
  waiting for transfers between devices: 396 us -> 0 us
  local copies, waits for them, and re-layouts: 28.7 us -> 0 us
  other arithmetic: 19.4 us -> 0 us
  between operations: 14.5 us -> 0.64 us
    pallas_call x0 -> x2, Pallas kernels: none -> 504 us  [the longest x1 493 us: step(): pl.pallas_call(kernel, out_shape=arrays(shapes), in_specs=[anywhere] * 5,...]
    dot_general x17 -> x0, matrix products: 422 us -> none  [the longest x6 149 us: layer(): up = jnp.dot(a, w['w_up'], preferred_element_type=jnp.float32)]
    reduce_scatter x6 -> x0, waiting for transfers between devices: 200 us -> none  [summed(): lax.psum_scatter(term, 's', scatter_dimension=0, tiled=True)]
    all_gather x6 -> x0, waiting for transfers between devices: 125 us -> none  [fetched(): lax.all_gather(w[number], 's', axis=0, tiled=True)]
    psum x1 -> x0, waiting for transfers between devices: 68.9 us -> none  [summed(): lax.psum(lax.psum_scatter(term, 's', scatter_dimension=0, tiled=True), 'r')]
    unnamed x33 -> x0, local copies, waits for them, and re-layouts: 21.9 us -> none
  transfers between devices with their start and end apart: 13 -> 0, of which waited for: 11 -> 0; matrix products, arithmetic and copies ran while one was open for 40% -> 0% of each run, Pallas kernels for 0% -> 0%
where the time goes in v2:
time: 506 us; the launch traced here: 505 us
  Pallas kernels  504 us (100%)
    pallas_call x1, Pallas kernels, step(): pl.pallas_call(kernel, out_shape=arrays(shapes), in_specs=[anywhere] * 5,...  493 us
    pallas_call x1, Pallas kernels, step(): pl.pallas_call(finish, out_shape=arrays(outs), in_specs=[anywhere] * 13,...  11.4 us

profile of v2, /device:TPU:0, one launch (start us, length us, event | category | flops | bytes accessed | tf_op | source)
XLA Modules:
  0.0 504.6 jit_solution(14455746855804231534)
XLA Ops:
  0.6 492.5 %step.1 = (bf16[2048,1024]{1,0:T(8,128)(2,1)}, bf16[1024,6400]{1,0:T(8,128)(2,1)}, bf16[1024,6400]{1,0:T(8,128)(2,1)}, bf16[3200,1024]{1,0:T(8,128)(2,1)}, bf16[...) custom-call(bf16[1,2048,1024]{2,1,0:T(8,128)(2,1)} %x.1, ...), custom_call_target="tpu_custom_call" | custom-call | flops 228170137600 | bytes 1073741824 | tf_op jit(solution)/shard_map/step/pallas_call | solution.py:600
  493.2 11.4 %finish.1 = (bf16[1,2048,1024]{2,1,0:T(8,128)(2,1)}, bf16[2,128,3200]{2,1,0:T(8,128)(2,1)}, bf16[2,128,3200]{2,1,0:T(8,128)(2,1)}, bf16[2,400,1024]{2,1,0:T(8,128)(2,1)}) custom-call(bf16[2048,1024]{1,0:T(8,128)(2,1)} %get-tuple-element.17.dx, f32[400,1024]{1,0:T(8,128)} %get-tuple-element.18.refs_0_, bf16[400,1024]{1,0:T(8,128)(2,1)} %get-tuple-element.19.refs_1_, ...), custom_call_target="tpu_custom_call" | custom-call | tf_op jit(solution)/shard_map/finish/pallas_call | solution.py:622
